TPU v7x, 32 devices: a whole 2x2x4 slice. The times are simulated.
32 devices in a mesh: row: 2 (over y), col: 4 (over z), layer: 4 (over x, core).
Axes of the slice: x: 2, y: 2, z: 4, core: 2. Of those that a mesh axis runs over, the one named last changes fastest.
Arguments:
- density_tiles: bfloat16 [192, 4, 2, 128, 128], P(('row', 'col')), may hold values from -1.5 to 1.5
- tile_columns: int32 [192, 4, 2], P(('row', 'col')), may hold values from -1 to 191, as said below
Outputs:
- square_tiles: bfloat16 [192, 4, 2, 128, 128], P(('row', 'col'), None, None, 'layer')
Inputs may be any that keep to these rules, and one draw needn't show every extreme that they name: `tile_columns`: entry [i, g, s] is a tile column in group g (columns g * 48 to (g + 1) * 48 - 1) or -1; within one block row and group the listed columns are distinct and empty slots come after the listed ones; block row i lists its own column i in the first slot of its group, whose 2 slots are all listed; other groups hold 0 to 2 listed tiles.
All inputs are finite; a program needn't handle non-finite values.
Results may differ from a plain program's by a relative error of at most 0.0048.
Values may be sent and summed in bfloat16 or wider, within the bound.
A program may use at most 128 MiB of HBM per device.

v0:
```python
import functools

import jax
import jax.numpy as jnp
from jax import lax
from jax.experimental import pallas as pl
from jax.experimental.pallas import tpu as pltpu
from jax.sharding import PartitionSpec as P

MESH = pl.DeviceIdType.MESH


def divisor(total, most):
    return max(d for d in range(1, most + 1) if total % d == 0)


def kernel(
    sizes, columns_ref, tiles_ref, meta_ref, out_ref,
    left, right, meta_all, meta_smem, stage,
    local_sem, meta_send, meta_recv, send_sem, recv_sem, out_send, out_recv,
):
    row_count, col_count, layer_count, chunks, out_chunks, is_balanced = sizes
    n, group_count, slots, tile, _ = tiles_ref.shape
    cells = row_count * col_count
    per_layer = group_count // layer_count
    quarter = tile // layer_count
    width = group_count * slots
    r, c, l = lax.axis_index("row"), lax.axis_index("col"), lax.axis_index("layer")
    me = r * col_count + c
    own_groups = pl.ds(l * per_layer, per_layer)

    own_copy = pltpu.make_async_copy(
        tiles_ref.at[:, own_groups], right.at[pl.ds(me * n, n)], local_sem.at[0]
    )
    left_copy = pltpu.make_async_copy(tiles_ref, left, local_sem.at[1])
    meta_copy = pltpu.make_async_copy(meta_ref, meta_all.at[pl.ds(me * n, n)], local_sem.at[2])
    own_copy.start()
    meta_copy.start()
    left_copy.start()
    right[cells * n] = jnp.zeros(right.shape[1:], right.dtype)

    def cell_id(offset):
        target = lax.rem(me + offset, cells)
        return {"row": lax.div(target, col_count), "col": lax.rem(target, col_count)}

    def layer_id(offset):
        return {"layer": lax.rem(l + offset, layer_count)}

    barrier = pltpu.get_barrier_semaphore()
    for offset in range(1, cells):
        pl.semaphore_signal(barrier, inc=1, device_id=cell_id(offset), device_id_type=MESH)
    for offset in range(1, layer_count):
        pl.semaphore_signal(barrier, inc=1, device_id=layer_id(offset), device_id_type=MESH)
    pl.semaphore_wait(barrier, cells - 1 + layer_count - 1)
    own_copy.wait()

    step_rows = n // chunks
    sent = []

    def rows_of(cell, chunk):
        return pl.ds(cell * n + chunk * step_rows, step_rows)

    def copy_of(cell, chunk, way, device):
        return pltpu.make_async_remote_copy(
            src_ref=right.at[rows_of(cell, chunk)],
            dst_ref=right.at[rows_of(cell, chunk)],
            send_sem=send_sem.at[way, cell, chunk],
            recv_sem=recv_sem.at[cell, chunk],
            device_id=device,
            device_id_type=MESH,
        )

    ways = {
        "up": (0, c < col_count - 1, {"col": jnp.minimum(c + 1, col_count - 1)}),
        "down": (1, c > 0, {"col": jnp.maximum(c - 1, 0)}),
        "south": (2, r < row_count - 1, {"row": jnp.minimum(r + 1, row_count - 1)}),
        "north": (3, r > 0, {"row": jnp.maximum(r - 1, 0)}),
    }

    def send(cell, chunk, way, condition=True):
        index, exists, device = ways[way]
        wanted = jnp.logical_and(exists, condition)

        @pl.when(wanted)
        def _():
            copy_of(cell, chunk, index, device).start()

        sent.append((wanted, cell, chunk, index, device))

    def await_arrival(cell, chunk):
        copy_of(cell, chunk, 0, {"col": c}).wait_recv()

    for chunk in range(chunks):
        for way in ("up", "down", "south", "north"):
            send(me, chunk, way)

    meta_copy.wait()
    meta_copies = []
    for offset in range(1, cells):
        copy = pltpu.make_async_remote_copy(
            src_ref=meta_ref,
            dst_ref=meta_all.at[pl.ds(me * n, n)],
            send_sem=meta_send.at[offset],
            recv_sem=meta_recv.at[offset],
            device_id=cell_id(offset),
            device_id_type=MESH,
        )
        copy.start()
        meta_copies.append(copy)

    even = lax.rem(c, 2) == 0
    for step in range(1, col_count):
        for chunk in range(chunks):
            for origin, has, way, is_pair in (
                (c - step, c >= step, "up", jnp.logical_not(even)),
                (c + step, c + step < col_count, "down", even),
            ):
                origin = jnp.clip(origin, 0, col_count - 1)
                cell = r * col_count + origin

                @pl.when(has)
                def _():
                    await_arrival(cell, chunk)

                send(cell, chunk, way, has)
                across = has
                if is_balanced and step == 1 and chunk >= chunks // 2:
                    across = jnp.logical_and(has, jnp.logical_not(is_pair))
                send(cell, chunk, "south", across)
                send(cell, chunk, "north", across)

    if is_balanced:
        other = (1 - r) * col_count + c
        for chunk in range(chunks):
            await_arrival(other, chunk)
            if chunk >= chunks // 2:
                send(other, chunk, "up", even)
                send(other, chunk, "down", jnp.logical_not(even))
        for step in range(1, col_count):
            origin = (1 - r) * col_count + lax.rem(c + step, col_count)
            for chunk in range(chunks):
                await_arrival(origin, chunk)
    else:
        for step in range(1, row_count):
            for shift in range(col_count):
                for chunk in range(chunks):
                    for origin, has, way in (
                        (r - step, r >= step, "south"),
                        (r + step, r + step < row_count, "north"),
                    ):
                        origin = jnp.clip(origin, 0, row_count - 1)
                        cell = origin * col_count + lax.rem(c + shift, col_count)

                        @pl.when(has)
                        def _():
                            await_arrival(cell, chunk)

                        send(cell, chunk, way, has)

    for copy in meta_copies:
        copy.wait()
    table_copy = pltpu.make_async_copy(meta_all, meta_smem, local_sem.at[3])
    table_copy.start()
    table_copy.wait()
    left_copy.wait()

    def one_row(i, carry):
        targets = [
            columns_ref[i * width + l * per_layer * slots + s] for s in range(per_layer * slots)
        ]
        strips = []
        for a in range(width):
            k = columns_ref[i * width + a]
            inner = jnp.maximum(k, 0)
            pieces = []
            for s in range(per_layer * slots):
                group = s // slots
                row_index = jnp.int32(cells * n)
                slot_index = jnp.int32(0)
                is_live = (k >= 0) & (targets[s] >= 0)
                for t in range(slots):
                    hit = (meta_smem[inner, 0, group * slots + t] == targets[s]) & is_live
                    row_index = jnp.where(hit, inner, row_index)
                    slot_index = jnp.where(hit, t, slot_index)
                pieces.append(right[row_index, group, slot_index])
            strips.append(jnp.concatenate(pieces, axis=1))
        rights = jnp.concatenate(strips, axis=0)
        lefts = jnp.concatenate(
            [left[i, a // slots, a % slots] for a in range(width)], axis=1
        )
        total = jnp.dot(lefts, rights, preferred_element_type=jnp.float32).astype(stage.dtype)
        for q in range(layer_count):
            for s in range(per_layer * slots):
                stage[q, i, s // slots, s % slots] = total[
                    q * quarter:(q + 1) * quarter, s * tile:(s + 1) * tile
                ]
        return carry

    out_rows = n // out_chunks

    def out_copies(chunk):
        rows = pl.ds(chunk * out_rows, out_rows)
        copies = []
        for offset in range(layer_count):
            q = lax.rem(l + offset, layer_count)
            if offset == 0:
                copies.append(pltpu.make_async_copy(
                    stage.at[q, rows], out_ref.at[rows, own_groups], out_send.at[0, chunk]
                ))
            else:
                copies.append(pltpu.make_async_remote_copy(
                    src_ref=stage.at[q, rows],
                    dst_ref=out_ref.at[rows, own_groups],
                    send_sem=out_send.at[offset, chunk],
                    recv_sem=out_recv.at[offset, chunk],
                    device_id=layer_id(offset),
                    device_id_type=MESH,
                ))
        return copies

    all_out = []
    for chunk in range(out_chunks + 1):
        if chunk < out_chunks:
            lax.fori_loop(chunk * out_rows, (chunk + 1) * out_rows, one_row, 0)
        if chunk > 0:
            copies = out_copies(chunk - 1)
            for copy in copies[1:] + copies[:1]:
                copy.start()
            all_out.extend(copies)

    for wanted, cell, chunk, index, device in sent:
        @pl.when(wanted)
        def _():
            copy_of(cell, chunk, index, device).wait_send()

    for copy in all_out:
        copy.wait()


def on_device(density_tiles, tile_columns):
    row_count = lax.axis_size("row")
    col_count = lax.axis_size("col")
    layer_count = lax.axis_size("layer")
    n, group_count, slots, tile, _ = density_tiles.shape
    cells = row_count * col_count
    per_layer = group_count // layer_count
    quarter = tile // layer_count
    kept = per_layer * slots
    chunks = divisor(n, 4)
    out_chunks = divisor(n, 4)
    is_balanced = row_count == 2 and col_count % 2 == 0 and chunks % 2 == 0
    own = lax.dynamic_slice_in_dim(tile_columns, lax.axis_index("layer") * per_layer, per_layer, 1)
    meta = jnp.pad(own.reshape(n, 1, kept), ((0, 0), (0, 0), (0, 128 - kept)), constant_values=-1)
    dtype = density_tiles.dtype
    sizes = (row_count, col_count, layer_count, chunks, out_chunks, is_balanced)
    return pl.pallas_call(
        functools.partial(kernel, sizes),
        out_shape=jax.ShapeDtypeStruct((n, group_count, slots, quarter, tile), dtype),
        in_specs=[
            pl.BlockSpec(memory_space=pltpu.SMEM),
            pl.BlockSpec(memory_space=pl.ANY),
            pl.BlockSpec(memory_space=pltpu.VMEM),
        ],
        out_specs=pl.BlockSpec(memory_space=pl.ANY),
        scratch_shapes=[
            pltpu.VMEM(density_tiles.shape, dtype),
            pltpu.VMEM((cells * n + 1, per_layer, slots, tile, tile), dtype),
            pltpu.VMEM((cells * n, 1, 128), jnp.int32),
            pltpu.SMEM((cells * n, 1, 128), jnp.int32),
            pltpu.VMEM((layer_count, n, per_layer, slots, quarter, tile), dtype),
            pltpu.SemaphoreType.DMA((4,)),
            pltpu.SemaphoreType.DMA((cells,)),
            pltpu.SemaphoreType.DMA((cells,)),
            pltpu.SemaphoreType.DMA((4, cells, chunks)),
            pltpu.SemaphoreType.DMA((cells, chunks)),
            pltpu.SemaphoreType.DMA((layer_count, out_chunks)),
            pltpu.SemaphoreType.DMA((layer_count, out_chunks)),
        ],
        compiler_params=pltpu.CompilerParams(
            collective_id=0, has_side_effects=True, vmem_limit_bytes=60 * 1024 * 1024
        ),
    )(tile_columns.reshape(-1), density_tiles, meta)


def paired_kernel(
    sizes, tiles_ref, meta_ref, out_ref,
    left, right, meta_all, meta_smem, stage,
    local_sem, meta_send, meta_recv, send_sem, recv_sem, left_send, left_recv, out_send, out_recv,
):
    col_count, layer_count, chunks, out_chunks = sizes
    n, group_count, slots, tile, _ = tiles_ref.shape
    cells = 2 * col_count
    per_layer = group_count // layer_count
    quarter = tile // layer_count
    width = group_count * slots
    r, c, l = lax.axis_index("row"), lax.axis_index("col"), lax.axis_index("layer")
    high, k = lax.div(l, 2), lax.rem(l, 2)
    me = r * col_count + c
    base = k * col_count + c
    is_home = k == r
    is_guest = jnp.logical_not(is_home)
    group = 2 * high + r
    own_groups = pl.ds(group * per_layer, per_layer)
    other_groups = pl.ds((2 * high + 1 - r) * per_layer, per_layer)
    facing = {"row": 1 - r}
    partner = {"layer": 2 * high + 1 - k}

    own_copy = pltpu.make_async_copy(
        tiles_ref.at[:, own_groups], right.at[pl.ds(me * n, n)], local_sem.at[0]
    )
    left_copy = pltpu.make_async_copy(tiles_ref, left, local_sem.at[1])
    meta_copy = pltpu.make_async_copy(meta_ref, meta_all.at[pl.ds(me * n, n)], local_sem.at[2])
    own_copy.start()
    meta_copy.start()

    @pl.when(is_home)
    def _():
        left_copy.start()

    right[cells * n] = jnp.zeros(right.shape[1:], right.dtype)

    def cell_id(offset):
        target = lax.rem(me + offset, cells)
        return {"row": lax.div(target, col_count), "col": lax.rem(target, col_count)}

    barrier = pltpu.get_barrier_semaphore()
    for offset in range(1, cells):
        pl.semaphore_signal(barrier, inc=1, device_id=cell_id(offset), device_id_type=MESH)
    for offset in range(1, layer_count):
        for row in (r, 1 - r):
            pl.semaphore_signal(
                barrier,
                inc=1,
                device_id={"row": row, "layer": lax.rem(l + offset, layer_count)},
                device_id_type=MESH,
            )
    pl.semaphore_wait(barrier, cells - 1 + 2 * (layer_count - 1))

    step_rows = n // chunks
    sent = []

    def rows_of(cell, chunk):
        return pl.ds(cell * n + chunk * step_rows, step_rows)

    def copy_of(cell, chunk, way, device):
        source = right.at[rows_of(cell, chunk)]
        if way == 3:
            source = tiles_ref.at[pl.ds(chunk * step_rows, step_rows), other_groups]
        return pltpu.make_async_remote_copy(
            src_ref=source,
            dst_ref=right.at[rows_of(cell, chunk)],
            send_sem=send_sem.at[way, cell, chunk],
            recv_sem=recv_sem.at[cell, chunk],
            device_id=device,
            device_id_type=MESH,
        )

    ways = {
        "up": (0, c < col_count - 1, {"col": jnp.minimum(c + 1, col_count - 1)}),
        "down": (1, c > 0, {"col": jnp.maximum(c - 1, 0)}),
        "partner": (2, True, partner),
        "facing": (3, True, facing),
    }

    def send(cell, chunk, way, condition):
        index, exists, device = ways[way]
        wanted = jnp.logical_and(exists, condition)

        @pl.when(wanted)
        def _():
            copy_of(cell, chunk, index, device).start()

        sent.append((wanted, cell, chunk, index, device))

    def await_arrival(cell, chunk, condition):
        @pl.when(condition)
        def _():
            copy_of(cell, chunk, 2, partner).wait_recv()

    for chunk in range(chunks):
        send(me, chunk, "facing", is_home)
    own_copy.wait()
    for chunk in range(chunks):
        for way in ("up", "down"):
            send(me, chunk, way, is_home)
    left_out = pltpu.make_async_remote_copy(
        src_ref=tiles_ref, dst_ref=left, send_sem=left_send, recv_sem=left_recv,
        device_id=facing, device_id_type=MESH,
    )

    meta_copy.wait()
    meta_copies = []
    for offset in range(1, cells):
        copy = pltpu.make_async_remote_copy(
            src_ref=meta_ref,
            dst_ref=meta_all.at[pl.ds(me * n, n)],
            send_sem=meta_send.at[offset],
            recv_sem=meta_recv.at[offset],
            device_id=cell_id(offset),
            device_id_type=MESH,
        )
        copy.start()
        meta_copies.append(copy)

    @pl.when(is_home)
    def _():
        left_out.start()

    for chunk in range(chunks):
        await_arrival(base, chunk, is_guest)
        for way in ("up", "down", "partner"):
            send(base, chunk, way, is_guest)

    for step in range(1, col_count):
        for chunk in range(chunks):
            for origin, has, way in (
                (c - step, c >= step, "up"),
                (c + step, c + step < col_count, "down"),
            ):
                cell = k * col_count + jnp.clip(origin, 0, col_count - 1)
                await_arrival(cell, chunk, has)
                send(cell, chunk, way, has)
                send(cell, chunk, "partner", has)

    for chunk in range(chunks):
        await_arrival((1 - k) * col_count + c, chunk, is_home)
    for step in range(1, col_count):
        cell = (1 - k) * col_count + lax.rem(c + step, col_count)
        for chunk in range(chunks):
            await_arrival(cell, chunk, True)

    for copy in meta_copies:
        copy.wait()
    table_copy = pltpu.make_async_copy(meta_all, meta_smem, local_sem.at[3])
    table_copy.start()
    table_copy.wait()

    @pl.when(is_home)
    def _():
        left_copy.wait()

    @pl.when(is_guest)
    def _():
        left_out.wait_recv()

    first = group * per_layer * slots

    def one_row(i, carry):
        block_row = base * n + i
        targets = [meta_smem[block_row, 0, first + s] for s in range(per_layer * slots)]
        strips = []
        for a in range(width):
            column = meta_smem[block_row, 0, a]
            inner = jnp.maximum(column, 0)
            pieces = []
            for s in range(per_layer * slots):
                part = s // slots
                row_index = jnp.int32(cells * n)
                slot_index = jnp.int32(0)
                is_live = (column >= 0) & (targets[s] >= 0)
                for t in range(slots):
                    hit = (meta_smem[inner, 0, first + part * slots + t] == targets[s]) & is_live
                    row_index = jnp.where(hit, inner, row_index)
                    slot_index = jnp.where(hit, t, slot_index)
                pieces.append(right[row_index, part, slot_index])
            strips.append(jnp.concatenate(pieces, axis=1))
        rights = jnp.concatenate(strips, axis=0)
        lefts = jnp.concatenate(
            [left[i, a // slots, a % slots] for a in range(width)], axis=1
        )
        total = jnp.dot(lefts, rights, preferred_element_type=jnp.float32).astype(stage.dtype)
        for q in range(layer_count):
            for s in range(per_layer * slots):
                stage[q, i, s // slots, s % slots] = total[
                    q * quarter:(q + 1) * quarter, s * tile:(s + 1) * tile
                ]
        return carry

    out_rows = n // out_chunks

    def out_copy(chunk, q, source):
        rows = pl.ds(chunk * out_rows, out_rows)
        return pltpu.make_async_remote_copy(
            src_ref=stage.at[q, rows],
            dst_ref=out_ref.at[rows, pl.ds(source * per_layer, per_layer)],
            send_sem=out_send.at[q, chunk],
            recv_sem=out_recv.at[source, chunk],
            device_id={"row": k, "layer": q},
            device_id_type=MESH,
        )

    def kept_copy(chunk):
        rows = pl.ds(chunk * out_rows, out_rows)
        return pltpu.make_async_copy(
            stage.at[l, rows], out_ref.at[rows, own_groups], out_send.at[l, chunk]
        )

    for chunk in range(out_chunks + 1):
        if chunk < out_chunks:
            lax.fori_loop(chunk * out_rows, (chunk + 1) * out_rows, one_row, 0)
        if chunk > 0:
            for offset in range(layer_count - 1, -1, -1):
                q = lax.rem(l + offset, layer_count)
                if offset:
                    out_copy(chunk - 1, q, group).start()
                else:
                    @pl.when(is_guest)
                    def _():
                        out_copy(chunk - 1, q, group).start()

                    @pl.when(is_home)
                    def _():
                        kept_copy(chunk - 1).start()

    for wanted, cell, chunk, index, device in sent:
        @pl.when(wanted)
        def _():
            copy_of(cell, chunk, index, device).wait_send()

    @pl.when(is_home)
    def _():
        left_out.wait_send()

    for chunk in range(out_chunks):
        for offset in range(layer_count):
            q = lax.rem(l + offset, layer_count)
            source = lax.rem(group + offset, layer_count)
            if offset:
                out_copy(chunk, q, source).wait()
            else:
                @pl.when(is_guest)
                def _():
                    out_copy(chunk, q, source).wait()

                @pl.when(is_home)
                def _():
                    kept_copy(chunk).wait()


def on_device_paired(density_tiles, tile_columns):
    col_count = lax.axis_size("col")
    layer_count = lax.axis_size("layer")
    n, group_count, slots, tile, _ = density_tiles.shape
    cells = 2 * col_count
    per_layer = group_count // layer_count
    quarter = tile // layer_count
    width = group_count * slots
    chunks = divisor(n, 2)
    out_chunks = divisor(n, 12)
    lanes = -(-width // 128) * 128
    meta = jnp.pad(
        tile_columns.reshape(n, 1, width), ((0, 0), (0, 0), (0, lanes - width)), constant_values=-1
    )
    dtype = density_tiles.dtype
    return pl.pallas_call(
        functools.partial(paired_kernel, (col_count, layer_count, chunks, out_chunks)),
        out_shape=jax.ShapeDtypeStruct((n, group_count, slots, quarter, tile), dtype),
        in_specs=[
            pl.BlockSpec(memory_space=pl.ANY),
            pl.BlockSpec(memory_space=pltpu.VMEM),
        ],
        out_specs=pl.BlockSpec(memory_space=pl.ANY),
        scratch_shapes=[
            pltpu.VMEM(density_tiles.shape, dtype),
            pltpu.VMEM((cells * n + 1, per_layer, slots, tile, tile), dtype),
            pltpu.VMEM((cells * n, 1, lanes), jnp.int32),
            pltpu.SMEM((cells * n, 1, lanes), jnp.int32),
            pltpu.VMEM((layer_count, n, per_layer, slots, quarter, tile), dtype),
            pltpu.SemaphoreType.DMA((4,)),
            pltpu.SemaphoreType.DMA((cells,)),
            pltpu.SemaphoreType.DMA((cells,)),
            pltpu.SemaphoreType.DMA((4, cells, chunks)),
            pltpu.SemaphoreType.DMA((cells, chunks)),
            pltpu.SemaphoreType.DMA,
            pltpu.SemaphoreType.DMA,
            pltpu.SemaphoreType.DMA((layer_count, out_chunks)),
            pltpu.SemaphoreType.DMA((layer_count, out_chunks)),
        ],
        compiler_params=pltpu.CompilerParams(
            collective_id=1, has_side_effects=True, vmem_limit_bytes=60 * 1024 * 1024
        ),
    )(density_tiles, meta)


def sparse_kernel(
    sizes, tiles_ref, meta_ref, out_ref, flag_ref,
    left, diag, extra, pack, stage, meta_all, meta_smem,
    send_list, send_smem, row_list, row_smem, flag_all,
    local_sem, meta_send, meta_recv, flag_send, flag_recv,
    main_send, main_recv, side_send, side_recv,
):
    row_count, col_count, layer_count, group_count, per_pair, per_row, padded = sizes
    n, width, tile, _ = tiles_ref.shape
    cells = row_count * col_count
    quarter = tile // layer_count
    entries = padded * width
    span = -(-(cells * n) // 128) * 128
    r, c, l = lax.axis_index("row"), lax.axis_index("col"), lax.axis_index("layer")
    x, k = lax.div(l, 2), lax.rem(l, 2)
    facing_layer = 2 * (1 - x) + k
    me = r * col_count + c
    own_slot = lax.div(me * n * group_count, cells * n) * (width // group_count)
    partner = {"layer": 2 * x + 1 - k}
    facing = {"layer": facing_layer}

    meta_copy = pltpu.make_async_copy(meta_ref, meta_all.at[me], local_sem.at[0])
    diag_copy = pltpu.make_async_copy(
        tiles_ref.at[:, own_slot], diag.at[pl.ds(me * n, n)], local_sem.at[1]
    )
    left_copy = pltpu.make_async_copy(tiles_ref, left, local_sem.at[2])
    table_copy = pltpu.make_async_copy(meta_ref, meta_smem, local_sem.at[3])
    diag_copy.start()
    meta_copy.start()
    table_copy.start()
    left_copy.start()

    def cell_id(cell):
        return {"row": lax.div(cell, col_count), "col": lax.rem(cell, col_count)}

    def other_cell(offset):
        return lax.rem(me + offset, cells)

    barrier = pltpu.get_barrier_semaphore()
    for offset in range(1, cells):
        pl.semaphore_signal(
            barrier, inc=1, device_id=cell_id(other_cell(offset)), device_id_type=MESH
        )
    for device in (partner, facing):
        pl.semaphore_signal(barrier, inc=1, device_id=device, device_id_type=MESH)
    pl.semaphore_wait(barrier, cells - 1 + 2)

    sent = []

    def remote(source, target, send, recv, device):
        return pltpu.make_async_remote_copy(
            src_ref=source, dst_ref=target, send_sem=send, recv_sem=recv,
            device_id=device, device_id_type=MESH,
        )

    def launch(copy, condition=True):
        if condition is True:
            copy.start()
        else:
            @pl.when(condition)
            def _():
                copy.start()
        sent.append((copy, condition))

    def await_recv(copy, condition=True):
        if condition is True:
            copy.wait_recv()
        else:
            @pl.when(condition)
            def _():
                copy.wait_recv()

    def part(kind, cell, q):
        buffer, count = ((diag, n), (extra, per_pair))[kind]
        return buffer.at[pl.ds(cell * count, count), pl.ds(q * quarter, quarter)]

    up = {"col": jnp.minimum(c + 1, col_count - 1)}
    down = {"col": jnp.maximum(c - 1, 0)}
    across = {"row": 1 - r}

    def line_copy(cell, way):
        device = (up, down, across)[way]
        piece = part(0, cell, l)
        return remote(piece, piece, main_send.at[0, way, cell], main_recv.at[0, cell], device)

    def side_copy(kind, cell, way):
        device = (partner, facing, partner)[way]
        piece = part(kind, cell, facing_layer if way == 2 else l)
        return remote(
            piece, piece, side_send.at[kind, way, cell], side_recv.at[kind, way, cell], device
        )

    diag_copy.wait()
    launch(line_copy(me, 0), c < col_count - 1)
    launch(line_copy(me, 1), c > 0)
    launch(line_copy(me, 2))
    meta_copies = []
    for offset in range(1, cells):
        copy = remote(
            meta_ref, meta_all.at[me], meta_send.at[offset], meta_recv.at[offset],
            cell_id(other_cell(offset)),
        )
        copy.start()
        meta_copies.append(copy)
    meta_copy.wait()
    for copy in meta_copies:
        copy.wait_recv()

    small_row = lax.broadcasted_iota(jnp.int32, (padded, 128), 0)
    small_lane = lax.broadcasted_iota(jnp.int32, (padded, 128), 1)
    wide_row = lax.broadcasted_iota(jnp.int32, (padded, span), 0)
    wide_lane = lax.broadcasted_iota(jnp.int32, (padded, span), 1)
    tall_row = lax.broadcasted_iota(jnp.int32, (span, 128), 0)
    entry_row = lax.broadcasted_iota(jnp.int32, (entries, 128), 0)
    entry_lane = lax.broadcasted_iota(jnp.int32, (entries, 128), 1).astype(jnp.float32)
    before = (
        lax.broadcasted_iota(jnp.int32, (entries, entries), 0)
        > lax.broadcasted_iota(jnp.int32, (entries, entries), 1)
    ).astype(jnp.float32).astype(jnp.bfloat16)
    ones = jnp.ones((128, 128), jnp.bfloat16)

    def dot(a, b):
        return jnp.dot(a, b, preferred_element_type=jnp.float32)

    def chosen(cell):
        columns = meta_all[cell, 0:padded]
        pieces = []
        for b in range(width):
            hit = (columns[:, b:b + 1] == wide_lane) & (wide_lane != wide_row + cell * n)
            pieces.append(jnp.where(hit, 1.0, 0.0))
        return jnp.concatenate(pieces, axis=0).astype(jnp.bfloat16)

    def listing(cell):
        rows = meta_all[cell, padded:padded + width]
        total = jnp.zeros((span, 128), jnp.float32)
        for a in range(width):
            total = jnp.where(rows[a:a + 1] == tall_row, a + 1.0, total)
        return total.astype(jnp.bfloat16)

    def inner_listing(source, cell):
        rows = meta_all[cell, padded:padded + width]
        total = jnp.zeros((padded, 128), jnp.float32)
        for a in range(width):
            total = jnp.where(rows[a:a + 1] == small_row + source * n, a + 1.0, total)
        total = jnp.where(small_row + source * n == small_lane + cell * n, 0.0, total)
        return jnp.concatenate([total] * width, axis=0)

    def matches(picked, listed, inner):
        goal = dot(picked, listed)
        hit = jnp.where((goal > 0) & (inner > 0), 1.0, 0.0)
        needed = jnp.where(dot(hit.astype(jnp.bfloat16), ones) > 0, 1.0, 0.0)
        rank = dot(before, needed.astype(jnp.bfloat16))
        return goal, hit, needed, rank

    lane_slot = lax.rem(entry_row, padded) * width + lax.div(entry_row, padded)
    slot_value = lane_slot.astype(jnp.float32)
    mine = chosen(me)

    def send_step(cell, carry):
        _, _, needed, rank = matches(mine, listing(cell), inner_listing(me, cell))
        picks = jnp.where((rank == entry_lane) & (needed > 0), slot_value, 0.0)
        send_list[pl.ds(cell, 1)] = jnp.sum(picks, axis=0, keepdims=True).astype(jnp.int32)
        return carry

    lax.fori_loop(0, cells, send_step, 0)
    send_copy = pltpu.make_async_copy(send_list, send_smem, local_sem.at[4])
    send_copy.start()
    send_copy.wait()
    left_copy.wait()

    def pack_step(m, carry):
        for offset in range(cells):
            cell = other_cell(offset)
            slot = jnp.clip(send_smem[cell, m], 0, n * width - 1)
            row, at = lax.div(slot, width), lax.rem(slot, width)
            if offset:
                pack[offset, m] = left[row, at, pl.ds(pl.multiple_of(l * quarter, quarter), quarter)]
            else:
                extra[me * per_pair + m] = left[row, at]
        return carry

    lax.fori_loop(0, per_pair, pack_step, 0)

    def extra_copy(offset, source):
        return remote(
            pack.at[offset], part(1, source, l), main_send.at[1, 0, offset],
            main_recv.at[1, source], cell_id(other_cell(offset)),
        )

    for offset in range(1, cells):
        launch(extra_copy(offset, me))

    def share(kind, cell, condition=True):
        launch(side_copy(kind, cell, 0), condition)
        launch(side_copy(kind, cell, 1), condition)

    line = []
    for step in range(1, col_count):
        line.append((c - step, c >= step, 0))
        line.append((c + step, c + step < col_count, 1))
    for origin, has, way in line:
        cell = r * col_count + jnp.clip(origin, 0, col_count - 1)
        await_recv(line_copy(cell, way), has)
        more = c < col_count - 1 if way == 0 else c > 0
        launch(line_copy(cell, way), jnp.logical_and(has, more))
        launch(line_copy(cell, 2), has)
        share(0, cell, has)
    beyond = [((1 - r) * col_count + c, True)]
    for origin, has, way in line:
        beyond.append(((1 - r) * col_count + jnp.clip(origin, 0, col_count - 1), has))
    for cell, has in beyond:
        await_recv(line_copy(cell, 2), has)
        share(0, cell, has)

    listed = listing(me)
    lists = -(-per_row // 8) * 8
    list_row = lax.broadcasted_iota(jnp.int32, (lists, 128), 0)

    def row_step(source, carry):
        held, running, most = carry
        inner = inner_listing(source, me)
        goal, hit, needed, rank = matches(chosen(source), listed, inner)
        place = dot(before, hit.astype(jnp.bfloat16)) + running
        value = ((rank + (source * per_pair).astype(jnp.float32)) * 16.0 + (inner - 1.0)) * 16.0 + goal
        value = value * hit
        for q in range(per_row):
            line_sum = jnp.sum(jnp.where(place == float(q), value, 0.0), axis=0, keepdims=True)
            held = held + jnp.where(list_row == q, line_sum, 0.0)
        running = running + jnp.sum(hit, axis=0, keepdims=True)
        most = jnp.maximum(most, jnp.max(rank + needed, axis=0, keepdims=True))
        return held, running, most

    zero = jnp.zeros((1, 128), jnp.float32)
    held, running, most = lax.fori_loop(
        0, cells, row_step, (jnp.zeros((lists, 128), jnp.float32), zero, zero)
    )
    row_list[...] = held.astype(jnp.int32)
    over = jnp.where((most > per_pair) | (running > per_row), 1, 0)
    flag_all[me] = jnp.broadcast_to(jnp.max(over), (8, 128))
    row_copy = pltpu.make_async_copy(row_list, row_smem, local_sem.at[5])
    row_copy.start()
    flag_copies = []
    for offset in range(1, cells):
        copy = remote(
            flag_all.at[me], flag_all.at[me], flag_send.at[offset], flag_recv.at[offset],
            cell_id(other_cell(offset)),
        )
        copy.start()
        flag_copies.append(copy)

    every = [other_cell(offset) for offset in range(1, cells)]

    def pass_on(kind, cell, condition=True):
        await_recv(side_copy(kind, cell, 1), condition)
        launch(side_copy(kind, cell, 2), condition)

    def settle(kind, cell):
        await_recv(side_copy(kind, cell, 0))
        await_recv(side_copy(kind, cell, 2))

    for cell in every:
        await_recv(extra_copy(1, cell))
        share(1, cell)
    for origin, has, way in line:
        pass_on(0, r * col_count + jnp.clip(origin, 0, col_count - 1), has)
    for cell, has in beyond:
        pass_on(0, cell, has)
    for cell in every:
        pass_on(1, cell)
    for cell in every:
        settle(0, cell)
        settle(1, cell)
    row_copy.wait()
    table_copy.wait()

    def one_row(i, carry):
        part_rows = pl.ds(pl.multiple_of(l * quarter, quarter), quarter)
        own = left[i, own_slot, part_rows]
        pieces = []
        for t in range(width):
            column = meta_smem[i, t]
            lower = diag[jnp.maximum(column, 0)]
            own_left = left[i, t, part_rows]
            own_left = jnp.where(own_slot == t, jnp.zeros_like(own_left), own_left)
            value = dot(
                jnp.concatenate([own, own_left], axis=1),
                jnp.concatenate([left[i, t], lower], axis=0),
            )
            pieces.append(jnp.where(column >= 0, value, 0.0))
        lefts = []
        rights = []
        for q in range(per_row):
            code = jnp.clip(row_smem[q, i], 0, cells * per_pair * 256 - 1)
            goal = lax.rem(code, 16)
            at = jnp.minimum(lax.rem(lax.div(code, 16), 16), width - 1)
            piece = left[i, at, part_rows]
            lefts.append(jnp.concatenate(
                [jnp.where(goal == t + 1, piece, jnp.zeros_like(piece)) for t in range(width)], axis=0
            ))
            rights.append(extra[lax.div(code, 256)])
        total = jnp.concatenate(pieces, axis=0) + dot(
            jnp.concatenate(lefts, axis=1), jnp.concatenate(rights, axis=0)
        )
        stage[i] = total.astype(stage.dtype).reshape(width, quarter, tile)
        return carry

    lax.fori_loop(0, n, one_row, 0)
    out_copy = pltpu.make_async_copy(stage, out_ref, local_sem.at[6])
    out_copy.start()
    for copy in flag_copies:
        copy.wait_recv()
    flag_ref[...] = jnp.max(flag_all[...], axis=0)
    for copy in meta_copies + flag_copies:
        copy.wait_send()
    for copy, condition in sent:
        if condition is True:
            copy.wait_send()
        else:
            @pl.when(condition)
            def _():
                copy.wait_send()
    out_copy.wait()


def on_device_sparse(density_tiles, tile_columns):
    row_count = lax.axis_size("row")
    col_count = lax.axis_size("col")
    layer_count = lax.axis_size("layer")
    n, group_count, slots, tile, _ = density_tiles.shape
    cells = row_count * col_count
    quarter = tile // layer_count
    width = group_count * slots
    per_pair, per_row = 16, 8
    padded = -(-n // 32) * 32
    dtype = density_tiles.dtype
    columns = tile_columns.reshape(n, width)
    meta = jnp.concatenate([
        jnp.pad(columns, ((0, padded - n), (0, 128 - width)), constant_values=-1),
        jnp.pad(columns.T, ((0, 0), (0, 128 - n)), constant_values=-1),
    ], axis=0)
    sizes = (row_count, col_count, layer_count, group_count, per_pair, per_row, padded)
    lists = -(-per_row // 8) * 8
    out, flag = pl.pallas_call(
        functools.partial(sparse_kernel, sizes),
        out_shape=(
            jax.ShapeDtypeStruct((n, width, quarter, tile), dtype),
            jax.ShapeDtypeStruct((8, 128), jnp.int32),
        ),
        in_specs=[
            pl.BlockSpec(memory_space=pl.ANY),
            pl.BlockSpec(memory_space=pltpu.VMEM),
        ],
        out_specs=(
            pl.BlockSpec(memory_space=pl.ANY),
            pl.BlockSpec(memory_space=pltpu.VMEM),
        ),
        scratch_shapes=[
            pltpu.VMEM((n, width, tile, tile), dtype),
            pltpu.VMEM((cells * n, tile, tile), dtype),
            pltpu.VMEM((cells * per_pair, tile, tile), dtype),
            pltpu.VMEM((cells, per_pair, quarter, tile), dtype),
            pltpu.VMEM((n, width, quarter, tile), dtype),
            pltpu.VMEM((cells, padded + width, 128), jnp.int32),
            pltpu.SMEM((padded + width, 128), jnp.int32),
            pltpu.VMEM((cells, 128), jnp.int32),
            pltpu.SMEM((cells, 128), jnp.int32),
            pltpu.VMEM((lists, 128), jnp.int32),
            pltpu.SMEM((lists, 128), jnp.int32),
            pltpu.VMEM((cells, 8, 128), jnp.int32),
            pltpu.SemaphoreType.DMA((7,)),
            pltpu.SemaphoreType.DMA((cells,)),
            pltpu.SemaphoreType.DMA((cells,)),
            pltpu.SemaphoreType.DMA((cells,)),
            pltpu.SemaphoreType.DMA((cells,)),
            pltpu.SemaphoreType.DMA((2, 3, cells)),
            pltpu.SemaphoreType.DMA((2, cells)),
            pltpu.SemaphoreType.DMA((2, 3, cells)),
            pltpu.SemaphoreType.DMA((2, 3, cells)),
        ],
        compiler_params=pltpu.CompilerParams(
            collective_id=2, has_side_effects=True, vmem_limit_bytes=60 * 1024 * 1024
        ),
    )(density_tiles.reshape(n, width, tile, tile), meta)
    out = out.reshape(n, group_count, slots, quarter, tile)
    return lax.cond(
        flag[0, 0] > 0,
        lambda: on_device_paired(density_tiles, tile_columns),
        lambda: out,
    )


def solution(mesh):
    paired = mesh.shape["row"] == 2 and mesh.shape["layer"] % 2 == 0
    four = paired and mesh.shape["layer"] == 4

    def on_each(density_tiles, tile_columns):
        n, group_count, slots, tile, _ = density_tiles.shape
        block_count = n * mesh.shape["row"] * mesh.shape["col"]
        fits = four and n % 8 == 0 and n <= 128 and group_count * slots <= 15 and slots > 0
        fits = fits and (block_count // group_count) % n == 0 and tile % 128 == 0
        fits = fits and mesh.shape["col"] <= 16
        if fits:
            return on_device_sparse(density_tiles, tile_columns)
        return (on_device_paired if paired else on_device)(density_tiles, tile_columns)

    in_specs = (P(("row", "col"), None, None, None, None), P(("row", "col"), None, None))
    out_specs = P(("row", "col"), None, None, "layer", None)
    return jax.shard_map(
        on_each, mesh=mesh, in_specs=in_specs, out_specs=out_specs, check_vma=False
    )
```

profile of v0, /device:TPU:1, one launch (start us, length us, event | category | flops | bytes accessed | tf_op | source)
XLA Modules:
  0.0 113.4 jit_solution(2306110625370341908)
XLA Ops:
  0.0 0.8 copy.9
  0.8 1.3 %select_add_fusion.meta_ref = s32[40,128]{1,0:T(8,128)} fusion(s32[8,24]{1,0:T(8,128)} %bitcast.10, s32[24,8]{1,0:T(8,128)S(1)} %copy.9), kind=kLoop, calls=%fused_computation | loop fusion | flops 25600 | bytes 22016 | tf_op jit(solution)/shard_map/concatenate | solution.py:921
  2.1 0.0 copy-start
  2.1 108.3 %shard_map.30 = (bf16[24,8,32,128]{3,2,1,0:T(8,128)(2,1)S(1)}, s32[8,128]{1,0:T(8,128)}) custom-call(bf16[24,8,128,128]{3,2,1,0:T(8,128)(2,1)} %bitcast.7, s32[40,128]{1,0:T(8,128)} %select_add_fusion.meta_ref), custom_call_target="tpu_custom_call" | custom-call | tf_op jit(solution)/shard_map/pallas_call | solution.py:927
  110.4 1.2 %slice.3 = s32[1,1]{1,0:T(1,128)} slice(s32[8,128]{1,0:T(8,128)} %get-tuple-element.19), slice={[0:1], [0:1]} | slice | bytes 8 | tf_op jit(solution)/shard_map/slice | solution.py:970
  112.2 0.0 copy-done
  112.3 1.1 %copy.14 = bf16[24,4,2,32,128]{4,3,2,1,0:T(8,128)(2,1)} copy(bf16[24,4,2,32,128]{4,3,2,1,0:T(8,128)(2,1)S(1)} %get-tuple-element.21) | data formatting | bytes 3145728
  (1 shorter events, 0.0 us)
Async XLA Ops:
  2.1 110.2 %copy-start = (s32[24,4,2]{0,2,1:T(2,128)S(1)}, s32[24,4,2]{0,2,1:T(2,128)}, u32[]{:S(2)}) copy-start(s32[24,4,2]{0,2,1:T(2,128)} %param.5) | copy-start | bytes 2308
where the time goes:
time: 114 us; the launch traced here: 113 us
  Pallas kernels  108 us (95%)
  local copies, waits for them, and re-layouts  3.09 us (3%)
  other arithmetic  1.3 us (1%)
    pallas_call x1, Pallas kernels, on_device_sparse(): pl.pallas_call(functools.partial(sparse_kernel, sizes), out_shape=(jax.Sh...  108 us

commit v1 on v0

--- a/solution.py
+++ b/solution.py
@@ -583,36 +583,39 @@
 
 
 def sparse_kernel(
-    sizes, tiles_ref, meta_ref, out_ref, flag_ref,
-    left, diag, extra, pack, stage, meta_all, meta_smem,
+    sizes, tiles_ref, columns_ref, out_ref, flag_ref,
+    left, diag, extra, lent, borrowed, pack, arrived, stage, total, needs, ranks, meta_own, meta_all, meta_smem,
     send_list, send_smem, row_list, row_smem, flag_all,
     local_sem, meta_send, meta_recv, flag_send, flag_recv,
-    main_send, main_recv, side_send, side_recv,
+    main_send, main_recv, side_send, side_recv, lent_sem, pack_send, pack_recv, extra_send, extra_recv,
 ):
-    row_count, col_count, layer_count, group_count, per_pair, per_row, padded = sizes
+    row_count, col_count, layer_count, group_count, per_row, padded = sizes
     n, width, tile, _ = tiles_ref.shape
+    per_lent, per_plane, pool = lent.shape[0], pack.shape[1], extra.shape[0]
     cells = row_count * col_count
     quarter = tile // layer_count
     entries = padded * width
     span = -(-(cells * n) // 128) * 128
+    lists = -(-per_row // 8) * 8
     r, c, l = lax.axis_index("row"), lax.axis_index("col"), lax.axis_index("layer")
     x, k = lax.div(l, 2), lax.rem(l, 2)
     facing_layer = 2 * (1 - x) + k
     me = r * col_count + c
+    opposite = (1 - r) * col_count + c
     own_slot = lax.div(me * n * group_count, cells * n) * (width // group_count)
     partner = {"layer": 2 * x + 1 - k}
     facing = {"layer": facing_layer}
 
-    meta_copy = pltpu.make_async_copy(meta_ref, meta_all.at[me], local_sem.at[0])
     diag_copy = pltpu.make_async_copy(
         tiles_ref.at[:, own_slot], diag.at[pl.ds(me * n, n)], local_sem.at[1]
     )
     left_copy = pltpu.make_async_copy(tiles_ref, left, local_sem.at[2])
-    table_copy = pltpu.make_async_copy(meta_ref, meta_smem, local_sem.at[3])
+    table_copy = pltpu.make_async_copy(meta_own, meta_smem, local_sem.at[3])
     diag_copy.start()
-    meta_copy.start()
-    table_copy.start()
     left_copy.start()
+    meta_own[...] = jnp.full(meta_own.shape, -1, jnp.int32)
+    meta_own[:, 0:n] = columns_ref[...]
+    meta_all[me] = meta_own[...]
 
     def cell_id(cell):
         return {"row": lax.div(cell, col_count), "col": lax.rem(cell, col_count)}
@@ -654,39 +657,40 @@
             def _():
                 copy.wait_recv()
 
-    def part(kind, cell, q):
-        buffer, count = ((diag, n), (extra, per_pair))[kind]
-        return buffer.at[pl.ds(cell * count, count), pl.ds(q * quarter, quarter)]
+    def part(cell, q):
+        return diag.at[pl.ds(cell * n, n), pl.ds(q * quarter, quarter)]
 
     up = {"col": jnp.minimum(c + 1, col_count - 1)}
     down = {"col": jnp.maximum(c - 1, 0)}
     across = {"row": 1 - r}
 
-    def line_copy(cell, way):
+    def line_copy(cell, way, wide=0):
         device = (up, down, across)[way]
-        piece = part(0, cell, l)
-        return remote(piece, piece, main_send.at[0, way, cell], main_recv.at[0, cell], device)
-
-    def side_copy(kind, cell, way):
+        piece = part(cell, facing_layer if wide else l)
+        return remote(
+            piece, piece, main_send.at[wide, way, cell], main_recv.at[wide, cell], device
+        )
+
+    def side_copy(cell, way):
         device = (partner, facing, partner)[way]
-        piece = part(kind, cell, facing_layer if way == 2 else l)
-        return remote(
-            piece, piece, side_send.at[kind, way, cell], side_recv.at[kind, way, cell], device
-        )
-
-    diag_copy.wait()
-    launch(line_copy(me, 0), c < col_count - 1)
-    launch(line_copy(me, 1), c > 0)
-    launch(line_copy(me, 2))
+        piece = part(cell, facing_layer if way == 2 else l)
+        return remote(piece, piece, side_send.at[way, cell], side_recv.at[way, cell], device)
+
     meta_copies = []
     for offset in range(1, cells):
         copy = remote(
-            meta_ref, meta_all.at[me], meta_send.at[offset], meta_recv.at[offset],
+            meta_own, meta_all.at[me], meta_send.at[offset], meta_recv.at[offset],
             cell_id(other_cell(offset)),
         )
         copy.start()
         meta_copies.append(copy)
-    meta_copy.wait()
+    diag_copy.wait()
+    has_up, has_down = c < col_count - 1, c > 0
+    launch(line_copy(me, 0), has_up)
+    launch(line_copy(me, 1), has_down)
+    launch(line_copy(me, 2))
+    launch(line_copy(me, 2, 1))
+    table_copy.start()
     for copy in meta_copies:
         copy.wait_recv()
 
@@ -707,7 +711,7 @@
         return jnp.dot(a, b, preferred_element_type=jnp.float32)
 
     def chosen(cell):
-        columns = meta_all[cell, 0:padded]
+        columns = jnp.transpose(meta_all[cell])[0:padded]
         pieces = []
         for b in range(width):
             hit = (columns[:, b:b + 1] == wide_lane) & (wide_lane != wide_row + cell * n)
@@ -715,112 +719,186 @@
         return jnp.concatenate(pieces, axis=0).astype(jnp.bfloat16)
 
     def listing(cell):
-        rows = meta_all[cell, padded:padded + width]
-        total = jnp.zeros((span, 128), jnp.float32)
+        rows = meta_all[cell]
+        weight = jnp.zeros((span, 128), jnp.float32)
         for a in range(width):
-            total = jnp.where(rows[a:a + 1] == tall_row, a + 1.0, total)
-        return total.astype(jnp.bfloat16)
+            weight = jnp.where(rows[a:a + 1] == tall_row, a + 1.0, weight)
+        return weight.astype(jnp.bfloat16)
 
     def inner_listing(source, cell):
-        rows = meta_all[cell, padded:padded + width]
-        total = jnp.zeros((padded, 128), jnp.float32)
+        rows = meta_all[cell]
+        weight = jnp.zeros((padded, 128), jnp.float32)
         for a in range(width):
-            total = jnp.where(rows[a:a + 1] == small_row + source * n, a + 1.0, total)
-        total = jnp.where(small_row + source * n == small_lane + cell * n, 0.0, total)
-        return jnp.concatenate([total] * width, axis=0)
+            weight = jnp.where(rows[a:a + 1] == small_row + source * n, a + 1.0, weight)
+        weight = jnp.where(small_row + source * n == small_lane + cell * n, 0.0, weight)
+        return jnp.concatenate([weight] * width, axis=0)
 
     def matches(picked, listed, inner):
         goal = dot(picked, listed)
         hit = jnp.where((goal > 0) & (inner > 0), 1.0, 0.0)
         needed = jnp.where(dot(hit.astype(jnp.bfloat16), ones) > 0, 1.0, 0.0)
-        rank = dot(before, needed.astype(jnp.bfloat16))
-        return goal, hit, needed, rank
-
-    lane_slot = lax.rem(entry_row, padded) * width + lax.div(entry_row, padded)
-    slot_value = lane_slot.astype(jnp.float32)
-    mine = chosen(me)
-
-    def send_step(cell, carry):
-        _, _, needed, rank = matches(mine, listing(cell), inner_listing(me, cell))
-        picks = jnp.where((rank == entry_lane) & (needed > 0), slot_value, 0.0)
-        send_list[pl.ds(cell, 1)] = jnp.sum(picks, axis=0, keepdims=True).astype(jnp.int32)
+        return goal, hit, needed
+
+    def rank_of(needed):
+        return dot(before, needed.astype(jnp.bfloat16))
+
+    def count_of(needed):
+        return jnp.sum(needed, axis=0, keepdims=True)
+
+    def picks_of(needed, rank, value):
+        chosen_values = jnp.where((rank == entry_lane) & (needed > 0), value, 0.0)
+        return jnp.sum(chosen_values, axis=0, keepdims=True)
+
+    slot_value = (
+        lax.rem(entry_row, padded) * width + lax.div(entry_row, padded)
+    ).astype(jnp.float32)
+    mine, theirs = chosen(me), chosen(opposite)
+    none = jnp.zeros((entries, 128), jnp.float32)
+    my_rows = pl.ds(pl.multiple_of(l * quarter, quarter), quarter)
+
+    def lent_step(at, wanted):
+        cell = (1 - r) * col_count + at
+        return jnp.maximum(wanted, matches(mine, listing(cell), inner_listing(me, cell))[2])
+
+    wanted = lax.fori_loop(0, col_count, lent_step, none, unroll=True)
+    send_list[0:1] = picks_of(wanted, rank_of(wanted), slot_value).astype(jnp.int32)
+    lent_most = count_of(wanted)
+    lent_list = pltpu.make_async_copy(send_list.at[0], send_smem.at[0], local_sem.at[4])
+    lent_list.start()
+    lent_list.wait()
+    left_copy.wait()
+
+    def own_piece(code):
+        code = jnp.clip(code, 0, n * width - 1)
+        return left[lax.div(code, width), lax.rem(code, width), my_rows]
+
+    def lent_pack(m, carry):
+        lent[m] = own_piece(send_smem[0, m])
         return carry
 
-    lax.fori_loop(0, cells, send_step, 0)
-    send_copy = pltpu.make_async_copy(send_list, send_smem, local_sem.at[4])
-    send_copy.start()
-    send_copy.wait()
-    left_copy.wait()
-
-    def pack_step(m, carry):
-        for offset in range(cells):
-            cell = other_cell(offset)
-            slot = jnp.clip(send_smem[cell, m], 0, n * width - 1)
-            row, at = lax.div(slot, width), lax.rem(slot, width)
+    lax.fori_loop(0, per_lent, lent_pack, 0, unroll=4)
+    lent_copy = remote(lent, borrowed, lent_sem.at[0], lent_sem.at[1], across)
+    launch(lent_copy)
+
+    def share(cell, condition=True, wide=False):
+        launch(side_copy(cell, 0), condition)
+        if not wide:
+            launch(side_copy(cell, 1), condition)
+
+    def take_line(cell, has, way, wide):
+        await_recv(line_copy(cell, way), has)
+        launch(line_copy(cell, way), jnp.logical_and(has, has_up if way == 0 else has_down))
+        share(cell, has, wide)
+        launch(line_copy(cell, 2), has)
+
+    line, beyond = [], []
+    for step in range(1, col_count):
+        for origin, has, way in ((c - step, c >= step, 0), (c + step, c + step < col_count, 1)):
+            origin = jnp.clip(origin, 0, col_count - 1)
+            line.append((r * col_count + origin, has, way, step == 1))
+            beyond.append(((1 - r) * col_count + origin, has))
+
+    for entry in line[:2]:
+        take_line(*entry)
+
+    def plane_step(at, wanted):
+        cell = r * col_count + at
+        listed = listing(cell)
+        own = matches(mine, listed, inner_listing(me, cell))[2]
+        send_list[pl.ds(8 + at, 1)] = picks_of(own, rank_of(own), slot_value).astype(jnp.int32)
+        their = matches(theirs, listed, inner_listing(opposite, cell))[2]
+        needs[at] = their
+        ranks[at] = rank_of(their) + count_of(own)
+        return jnp.maximum(wanted, their)
+
+    wanted = lax.fori_loop(0, col_count, plane_step, none, unroll=True)
+    borrowed_value = rank_of(wanted) + float(n * width)
+
+    def plane_finish(at, carry):
+        picks = picks_of(needs[at], ranks[at], borrowed_value).astype(jnp.int32)
+        send_list[pl.ds(8 + at, 1)] += picks
+        return carry
+
+    lax.fori_loop(0, col_count, plane_finish, 0, unroll=True)
+    rows_used = send_list.shape[0] - 8
+    plane_list = pltpu.make_async_copy(
+        send_list.at[pl.ds(8, rows_used)], send_smem.at[pl.ds(8, rows_used)], local_sem.at[4]
+    )
+    plane_list.start()
+
+    await_recv(line_copy(opposite, 2))
+    share(opposite, True, True)
+    await_recv(line_copy(opposite, 2, 1))
+    launch(side_copy(opposite, 2))
+    plane_list.wait()
+    await_recv(lent_copy)
+
+    def plane_piece(at, m):
+        code = send_smem[8 + at, m]
+        loaned = borrowed[jnp.clip(code - n * width, 0, per_lent - 1)]
+        return jnp.where(code < n * width, own_piece(code), loaned)
+
+    def plane_pack(m, carry):
+        for offset in range(col_count):
+            at = lax.rem(c + offset, col_count)
             if offset:
-                pack[offset, m] = left[row, at, pl.ds(pl.multiple_of(l * quarter, quarter), quarter)]
+                pack[offset, m] = plane_piece(at, m)
             else:
-                extra[me * per_pair + m] = left[row, at]
+                arrived[c, m] = plane_piece(at, m)
         return carry
 
-    lax.fori_loop(0, per_pair, pack_step, 0)
-
-    def extra_copy(offset, source):
+    lax.fori_loop(0, per_plane, plane_pack, 0, unroll=2)
+
+    def pack_copy(offset, origin):
         return remote(
-            pack.at[offset], part(1, source, l), main_send.at[1, 0, offset],
-            main_recv.at[1, source], cell_id(other_cell(offset)),
-        )
-
-    for offset in range(1, cells):
-        launch(extra_copy(offset, me))
-
-    def share(kind, cell, condition=True):
-        launch(side_copy(kind, cell, 0), condition)
-        launch(side_copy(kind, cell, 1), condition)
-
-    line = []
-    for step in range(1, col_count):
-        line.append((c - step, c >= step, 0))
-        line.append((c + step, c + step < col_count, 1))
-    for origin, has, way in line:
-        cell = r * col_count + jnp.clip(origin, 0, col_count - 1)
-        await_recv(line_copy(cell, way), has)
-        more = c < col_count - 1 if way == 0 else c > 0
-        launch(line_copy(cell, way), jnp.logical_and(has, more))
-        launch(line_copy(cell, 2), has)
-        share(0, cell, has)
-    beyond = [((1 - r) * col_count + c, True)]
-    for origin, has, way in line:
-        beyond.append(((1 - r) * col_count + jnp.clip(origin, 0, col_count - 1), has))
-    for cell, has in beyond:
+            pack.at[offset], arrived.at[origin], pack_send.at[offset], pack_recv.at[origin],
+            {"col": lax.rem(c + offset, col_count)},
+        )
+
+    for offset in range(1, col_count):
+        launch(pack_copy(offset, c))
+    launch(line_copy(me, 0, 1), has_up)
+    launch(line_copy(me, 1, 1), has_down)
+
+    def take_beyond(cell, has):
         await_recv(line_copy(cell, 2), has)
-        share(0, cell, has)
+        share(cell, has)
+
+    for entry in line[2:4]:
+        take_line(*entry)
+    for entry in beyond[:2]:
+        take_beyond(*entry)
 
     listed = listing(me)
-    lists = -(-per_row // 8) * 8
-    list_row = lax.broadcasted_iota(jnp.int32, (lists, 128), 0)
-
-    def row_step(source, carry):
-        held, running, most = carry
+    list_row = lax.broadcasted_iota(jnp.int32, (lists + 8, 128), 0)
+
+    def row_step(at, carry):
+        held, running, pooled, in_plane, most = carry
+        plane, far = lax.div(at, 2), lax.rem(at, 2)
+        source = jnp.where(far == 0, r, 1 - r) * col_count + plane
+        in_plane = jnp.where(far == 0, 0.0, in_plane)
         inner = inner_listing(source, me)
-        goal, hit, needed, rank = matches(chosen(source), listed, inner)
+        goal, hit, needed = matches(chosen(source), listed, inner)
+        rank = rank_of(needed)
         place = dot(before, hit.astype(jnp.bfloat16)) + running
-        value = ((rank + (source * per_pair).astype(jnp.float32)) * 16.0 + (inner - 1.0)) * 16.0 + goal
-        value = value * hit
+        value = (((rank + pooled) * 16.0 + (inner - 1.0)) * 16.0 + goal) * hit
         for q in range(per_row):
             line_sum = jnp.sum(jnp.where(place == float(q), value, 0.0), axis=0, keepdims=True)
             held = held + jnp.where(list_row == q, line_sum, 0.0)
-        running = running + jnp.sum(hit, axis=0, keepdims=True)
-        most = jnp.maximum(most, jnp.max(rank + needed, axis=0, keepdims=True))
-        return held, running, most
+        spot = rank + in_plane + (plane * per_plane).astype(jnp.float32)
+        held = held + jnp.where(list_row == lists, picks_of(needed, rank + pooled, spot), 0.0)
+        count = count_of(needed)
+        in_plane = in_plane + count
+        return held, running + count_of(hit), pooled + count, in_plane, jnp.maximum(most, in_plane)
 
     zero = jnp.zeros((1, 128), jnp.float32)
-    held, running, most = lax.fori_loop(
-        0, cells, row_step, (jnp.zeros((lists, 128), jnp.float32), zero, zero)
+    held, running, pooled, _, most = lax.fori_loop(
+        0, cells, row_step, (jnp.zeros((lists + 8, 128), jnp.float32), zero, zero, zero, zero),
+        unroll=2,
     )
     row_list[...] = held.astype(jnp.int32)
-    over = jnp.where((most > per_pair) | (running > per_row), 1, 0)
-    flag_all[me] = jnp.broadcast_to(jnp.max(over), (8, 128))
+    over = (most > per_plane) | (running > per_row) | (pooled > pool) | (lent_most > per_lent)
+    flag_all[me] = jnp.broadcast_to(jnp.max(jnp.where(over, 1, 0)), (8, 128))
     row_copy = pltpu.make_async_copy(row_list, row_smem, local_sem.at[5])
     row_copy.start()
     flag_copies = []
@@ -832,63 +910,87 @@
         copy.start()
         flag_copies.append(copy)
 
-    every = [other_cell(offset) for offset in range(1, cells)]
-
-    def pass_on(kind, cell, condition=True):
-        await_recv(side_copy(kind, cell, 1), condition)
-        launch(side_copy(kind, cell, 2), condition)
-
-    def settle(kind, cell):
-        await_recv(side_copy(kind, cell, 0))
-        await_recv(side_copy(kind, cell, 2))
-
-    for cell in every:
-        await_recv(extra_copy(1, cell))
-        share(1, cell)
-    for origin, has, way in line:
-        pass_on(0, r * col_count + jnp.clip(origin, 0, col_count - 1), has)
+    def pass_on(cell, condition=True):
+        await_recv(side_copy(cell, 1), condition)
+        launch(side_copy(cell, 2), condition)
+
+    def take_wide(cell, has, way, wide):
+        await_recv(line_copy(cell, way, 1), has)
+        launch(side_copy(cell, 2), has)
+
+    for entry in line[4:]:
+        take_line(*entry)
+    for entry in beyond[2:]:
+        take_beyond(*entry)
+    for entry in line[:2]:
+        take_wide(*entry)
+    row_copy.wait()
+    for offset in range(1, col_count):
+        await_recv(pack_copy(offset, lax.rem(c + offset, col_count)))
+
+    def pool_pack(m, carry):
+        code = jnp.clip(row_smem[lists, m], 0, col_count * per_plane - 1)
+        extra[m, my_rows] = arrived[lax.div(code, per_plane), lax.rem(code, per_plane)]
+        return carry
+
+    lax.fori_loop(0, pool, pool_pack, 0, unroll=4)
+
+    def extra_copy(way):
+        device = (partner, facing, partner)[way]
+        piece = extra.at[:, pl.ds((facing_layer if way == 2 else l) * quarter, quarter)]
+        return remote(piece, piece, extra_send.at[way], extra_recv.at[way], device)
+
+    launch(extra_copy(0))
+    launch(extra_copy(1))
+    for cell, has, _, _ in line[2:]:
+        pass_on(cell, has)
     for cell, has in beyond:
-        pass_on(0, cell, has)
-    for cell in every:
-        pass_on(1, cell)
-    for cell in every:
-        settle(0, cell)
-        settle(1, cell)
-    row_copy.wait()
+        pass_on(cell, has)
+    for offset in range(1, cells):
+        await_recv(side_copy(other_cell(offset), 0))
+        await_recv(side_copy(other_cell(offset), 2))
     table_copy.wait()
 
-    def one_row(i, carry):
-        part_rows = pl.ds(pl.multiple_of(l * quarter, quarter), quarter)
-        own = left[i, own_slot, part_rows]
+    def near_row(i, carry):
+        own = left[i, own_slot, my_rows]
         pieces = []
         for t in range(width):
-            column = meta_smem[i, t]
+            column = meta_smem[t, i]
             lower = diag[jnp.maximum(column, 0)]
-            own_left = left[i, t, part_rows]
+            own_left = left[i, t, my_rows]
             own_left = jnp.where(own_slot == t, jnp.zeros_like(own_left), own_left)
             value = dot(
                 jnp.concatenate([own, own_left], axis=1),
                 jnp.concatenate([left[i, t], lower], axis=0),
             )
             pieces.append(jnp.where(column >= 0, value, 0.0))
-        lefts = []
-        rights = []
+        total[i] = jnp.concatenate(pieces, axis=0)
+        return carry
+
+    lax.fori_loop(0, n, near_row, 0, unroll=2)
+    await_recv(extra_copy(1))
+    launch(extra_copy(2))
+    await_recv(extra_copy(0))
+    await_recv(extra_copy(2))
+
+    def far_row(i, carry):
+        lefts, rights = [], []
         for q in range(per_row):
-            code = jnp.clip(row_smem[q, i], 0, cells * per_pair * 256 - 1)
+            code = jnp.clip(row_smem[q, i], 0, pool * 256 - 1)
             goal = lax.rem(code, 16)
             at = jnp.minimum(lax.rem(lax.div(code, 16), 16), width - 1)
-            piece = left[i, at, part_rows]
+            piece = left[i, at, my_rows]
             lefts.append(jnp.concatenate(
                 [jnp.where(goal == t + 1, piece, jnp.zeros_like(piece)) for t in range(width)], axis=0
             ))
             rights.append(extra[lax.div(code, 256)])
-        total = jnp.concatenate(pieces, axis=0) + dot(
+        value = total[i] + dot(
             jnp.concatenate(lefts, axis=1), jnp.concatenate(rights, axis=0)
         )
-        stage[i] = total.astype(stage.dtype).reshape(width, quarter, tile)
+        stage[i] = value.astype(stage.dtype).reshape(width, quarter, tile)
         return carry
 
-    lax.fori_loop(0, n, one_row, 0)
+    lax.fori_loop(0, n, far_row, 0, unroll=4)
     out_copy = pltpu.make_async_copy(stage, out_ref, local_sem.at[6])
     out_copy.start()
     for copy in flag_copies:
@@ -914,16 +1016,12 @@
     cells = row_count * col_count
     quarter = tile // layer_count
     width = group_count * slots
-    per_pair, per_row = 16, 8
+    per_lent, per_plane, pool, per_row = 32, 24, 56, 8
     padded = -(-n // 32) * 32
     dtype = density_tiles.dtype
-    columns = tile_columns.reshape(n, width)
-    meta = jnp.concatenate([
-        jnp.pad(columns, ((0, padded - n), (0, 128 - width)), constant_values=-1),
-        jnp.pad(columns.T, ((0, 0), (0, 128 - n)), constant_values=-1),
-    ], axis=0)
-    sizes = (row_count, col_count, layer_count, group_count, per_pair, per_row, padded)
+    sizes = (row_count, col_count, layer_count, group_count, per_row, padded)
     lists = -(-per_row // 8) * 8
+    planes = -(-col_count // 8) * 8
     out, flag = pl.pallas_call(
         functools.partial(sparse_kernel, sizes),
         out_shape=(
@@ -941,15 +1039,22 @@
         scratch_shapes=[
             pltpu.VMEM((n, width, tile, tile), dtype),
             pltpu.VMEM((cells * n, tile, tile), dtype),
-            pltpu.VMEM((cells * per_pair, tile, tile), dtype),
-            pltpu.VMEM((cells, per_pair, quarter, tile), dtype),
+            pltpu.VMEM((pool, tile, tile), dtype),
+            pltpu.VMEM((per_lent, quarter, tile), dtype),
+            pltpu.VMEM((per_lent, quarter, tile), dtype),
+            pltpu.VMEM((col_count, per_plane, quarter, tile), dtype),
+            pltpu.VMEM((col_count, per_plane, quarter, tile), dtype),
             pltpu.VMEM((n, width, quarter, tile), dtype),
-            pltpu.VMEM((cells, padded + width, 128), jnp.int32),
-            pltpu.SMEM((padded + width, 128), jnp.int32),
-            pltpu.VMEM((cells, 128), jnp.int32),
-            pltpu.SMEM((cells, 128), jnp.int32),
-            pltpu.VMEM((lists, 128), jnp.int32),
-            pltpu.SMEM((lists, 128), jnp.int32),
+            pltpu.VMEM((n, width * quarter, tile), jnp.float32),
+            pltpu.VMEM((col_count, padded * width, 128), jnp.float32),
+            pltpu.VMEM((col_count, padded * width, 128), jnp.float32),
+            pltpu.VMEM((width, 128), jnp.int32),
+            pltpu.VMEM((cells, width, 128), jnp.int32),
+            pltpu.SMEM((width, 128), jnp.int32),
+            pltpu.VMEM((8 + planes, 128), jnp.int32),
+            pltpu.SMEM((8 + planes, 128), jnp.int32),
+            pltpu.VMEM((lists + 8, 128), jnp.int32),
+            pltpu.SMEM((lists + 8, 128), jnp.int32),
             pltpu.VMEM((cells, 8, 128), jnp.int32),
             pltpu.SemaphoreType.DMA((7,)),
             pltpu.SemaphoreType.DMA((cells,)),
@@ -958,13 +1063,18 @@
             pltpu.SemaphoreType.DMA((cells,)),
             pltpu.SemaphoreType.DMA((2, 3, cells)),
             pltpu.SemaphoreType.DMA((2, cells)),
-            pltpu.SemaphoreType.DMA((2, 3, cells)),
-            pltpu.SemaphoreType.DMA((2, 3, cells)),
+            pltpu.SemaphoreType.DMA((3, cells)),
+            pltpu.SemaphoreType.DMA((3, cells)),
+            pltpu.SemaphoreType.DMA((2,)),
+            pltpu.SemaphoreType.DMA((col_count,)),
+            pltpu.SemaphoreType.DMA((col_count,)),
+            pltpu.SemaphoreType.DMA((3,)),
+            pltpu.SemaphoreType.DMA((3,)),
         ],
         compiler_params=pltpu.CompilerParams(
             collective_id=2, has_side_effects=True, vmem_limit_bytes=60 * 1024 * 1024
         ),
-    )(density_tiles.reshape(n, width, tile, tile), meta)
+    )(density_tiles.reshape(n, width, tile, tile), tile_columns.reshape(n, width).T)
     out = out.reshape(n, group_count, slots, quarter, tile)
     return lax.cond(
         flag[0, 0] > 0,

time: 114 us -> 81.4 us (0.71)
  Pallas kernels: 108 us -> 78.1 us
  other arithmetic: 1.3 us -> 0 us
    pallas_call x1, Pallas kernels: 108 us -> 78.1 us  [on_device_sparse(): pl.pallas_call(functools.partial(sparse_kernel, sizes), out_shape=(jax.Sh...]
    concatenate x1 -> x0, other arithmetic: 1.3 us -> none  [on_device_sparse(): jnp.concatenate([jnp.pad(columns, ((0, padded - n), (0, 128 - width)), co...]
where the time goes in v1:
time: 81.4 us; the launch traced here: 81.2 us
  Pallas kernels  78.1 us (96%)
  local copies, waits for them, and re-layouts  2.33 us (3%)
    pallas_call x1, Pallas kernels, on_device_sparse(): pl.pallas_call(functools.partial(sparse_kernel, sizes), out_shape=(jax.Sh...  78.1 us

profile of v1, /device:TPU:1, one launch (start us, length us, event | category | flops | bytes accessed | tf_op | source)
XLA Modules:
  0.0 81.2 jit_solution(1643210869998857588)
XLA Ops:
  0.0 0.0 copy-start
  0.0 78.1 %shard_map.30 = (bf16[24,8,32,128]{3,2,1,0:T(8,128)(2,1)S(1)}, s32[8,128]{1,0:T(8,128)}) custom-call(bf16[24,8,128,128]{3,2,1,0:T(8,128)(2,1)} %bitcast.7, s32[8,24]{1,0:T(8,128)} %bitcast.9), custom_call_target="tpu_custom_call" | custom-call | tf_op jit(solution)/shard_map/pallas_call | solution.py:1025
  78.1 1.2 %slice.3 = s32[1,1]{1,0:T(1,128)} slice(s32[8,128]{1,0:T(8,128)} %get-tuple-element.19), slice={[0:1], [0:1]} | slice | bytes 8 | tf_op jit(solution)/shard_map/slice | solution.py:1080
  80.0 0.0 copy-done
  80.0 1.1 %copy.11 = bf16[24,4,2,32,128]{4,3,2,1,0:T(8,128)(2,1)} copy(bf16[24,4,2,32,128]{4,3,2,1,0:T(8,128)(2,1)S(1)} %get-tuple-element.21) | data formatting | bytes 3145728
  (1 shorter events, 0.0 us)
Async XLA Ops:
  0.0 80.0 %copy-start = (s32[24,4,2]{0,2,1:T(2,128)S(1)}, s32[24,4,2]{0,2,1:T(2,128)}, u32[]{:S(2)}) copy-start(s32[24,4,2]{0,2,1:T(2,128)} %param.5) | copy-start | bytes 2308

commit v2 on v1

--- a/solution.py
+++ b/solution.py
@@ -689,7 +689,6 @@
     launch(line_copy(me, 0), has_up)
     launch(line_copy(me, 1), has_down)
     launch(line_copy(me, 2))
-    launch(line_copy(me, 2, 1))
     table_copy.start()
     for copy in meta_copies:
         copy.wait_recv()
@@ -801,6 +800,10 @@
     for entry in line[:2]:
         take_line(*entry)
 
+    for entry in line[2:4]:
+        take_line(*entry)
+    launch(line_copy(me, 2, 1))
+
     def plane_step(at, wanted):
         cell = r * col_count + at
         listed = listing(cell)
@@ -828,8 +831,6 @@
 
     await_recv(line_copy(opposite, 2))
     share(opposite, True, True)
-    await_recv(line_copy(opposite, 2, 1))
-    launch(side_copy(opposite, 2))
     plane_list.wait()
     await_recv(lent_copy)
 
@@ -855,16 +856,14 @@
             {"col": lax.rem(c + offset, col_count)},
         )
 
-    for offset in range(1, col_count):
+    for offset in sorted(range(1, col_count), key=lambda o: abs(2 * o - col_count)):
         launch(pack_copy(offset, c))
-    launch(line_copy(me, 0, 1), has_up)
-    launch(line_copy(me, 1, 1), has_down)
 
     def take_beyond(cell, has):
         await_recv(line_copy(cell, 2), has)
         share(cell, has)
 
-    for entry in line[2:4]:
+    for entry in line[4:]:
         take_line(*entry)
     for entry in beyond[:2]:
         take_beyond(*entry)
@@ -918,12 +917,10 @@
         await_recv(line_copy(cell, way, 1), has)
         launch(side_copy(cell, 2), has)
 
-    for entry in line[4:]:
-        take_line(*entry)
     for entry in beyond[2:]:
         take_beyond(*entry)
-    for entry in line[:2]:
-        take_wide(*entry)
+    launch(line_copy(me, 0, 1), has_up)
+    launch(line_copy(me, 1, 1), has_down)
     row_copy.wait()
     for offset in range(1, col_count):
         await_recv(pack_copy(offset, lax.rem(c + offset, col_count)))
@@ -942,6 +939,10 @@
 
     launch(extra_copy(0))
     launch(extra_copy(1))
+    for entry in line[:2]:
+        take_wide(*entry)
+    await_recv(line_copy(opposite, 2, 1))
+    launch(side_copy(opposite, 2))
     for cell, has, _, _ in line[2:]:
         pass_on(cell, has)
     for cell, has in beyond:
@@ -990,12 +991,12 @@
         stage[i] = value.astype(stage.dtype).reshape(width, quarter, tile)
         return carry
 
-    lax.fori_loop(0, n, far_row, 0, unroll=4)
+    lax.fori_loop(0, n, far_row, 0, unroll=8)
     out_copy = pltpu.make_async_copy(stage, out_ref, local_sem.at[6])
     out_copy.start()
     for copy in flag_copies:
         copy.wait_recv()
-    flag_ref[...] = jnp.max(flag_all[...], axis=0)
+    flag_ref[0, 0] = jnp.max(flag_all[...])
     for copy in meta_copies + flag_copies:
         copy.wait_send()
     for copy, condition in sent:
@@ -1026,7 +1027,7 @@
         functools.partial(sparse_kernel, sizes),
         out_shape=(
             jax.ShapeDtypeStruct((n, width, quarter, tile), dtype),
-            jax.ShapeDtypeStruct((8, 128), jnp.int32),
+            jax.ShapeDtypeStruct((1, 1), jnp.int32),
         ),
         in_specs=[
             pl.BlockSpec(memory_space=pl.ANY),
@@ -1034,7 +1035,7 @@
         ],
         out_specs=(
             pl.BlockSpec(memory_space=pl.ANY),
-            pl.BlockSpec(memory_space=pltpu.VMEM),
+            pl.BlockSpec(memory_space=pltpu.SMEM),
         ),
         scratch_shapes=[
             pltpu.VMEM((n, width, tile, tile), dtype),

time: 81.4 us -> 60.1 us (0.74)
  Pallas kernels: 78.1 us -> 57.7 us
  local copies, waits for them, and re-layouts: 2.33 us -> 1.15 us
    pallas_call x1, Pallas kernels: 78.1 us -> 57.7 us  [on_device_sparse(): pl.pallas_call(functools.partial(sparse_kernel, sizes), out_shape=(jax.Sh...]
    slice x1 -> x0, local copies, waits for them, and re-layouts: 1.19 us -> none  [on_device_sparse(): flag[0, 0] > 0]
where the time goes in v2:
time: 60.1 us; the launch traced here: 59.5 us
  Pallas kernels  57.7 us (96%)
  local copies, waits for them, and re-layouts  1.15 us (2%)
  between operations  0.63 us (1%)
    pallas_call x1, Pallas kernels, on_device_sparse(): pl.pallas_call(functools.partial(sparse_kernel, sizes), out_shape=(jax.Sh...  57.7 us

profile of v2, /device:TPU:1, one launch (start us, length us, event | category | flops | bytes accessed | tf_op | source)
XLA Modules:
  0.0 59.5 jit_solution(13195756066808561713)
XLA Ops:
  0.0 0.0 copy-start
  0.0 57.7 %shard_map.30 = (bf16[24,8,32,128]{3,2,1,0:T(8,128)(2,1)S(1)}, s32[1,1]{1,0:T(1,128)}) custom-call(bf16[24,8,128,128]{3,2,1,0:T(8,128)(2,1)} %bitcast.7, s32[8,24]{1,0:T(8,128)} %bitcast.9), custom_call_target="tpu_custom_call" | custom-call | tf_op jit(solution)/shard_map/pallas_call | solution.py:1026
  58.3 0.0 copy-done
  58.3 1.1 %copy.11 = bf16[24,4,2,32,128]{4,3,2,1,0:T(8,128)(2,1)} copy(bf16[24,4,2,32,128]{4,3,2,1,0:T(8,128)(2,1)S(1)} %get-tuple-element.21) | data formatting | bytes 3145728
  (1 shorter events, 0.0 us)
Async XLA Ops:
  0.0 58.3 %copy-start = (s32[24,4,2]{0,2,1:T(2,128)S(1)}, s32[24,4,2]{0,2,1:T(2,128)}, u32[]{:S(2)}) copy-start(s32[24,4,2]{0,2,1:T(2,128)} %param.5) | copy-start | bytes 2308

commit v3 on v2

--- a/solution.py
+++ b/solution.py
@@ -587,7 +587,7 @@
     left, diag, extra, lent, borrowed, pack, arrived, stage, total, needs, ranks, meta_own, meta_all, meta_smem,
     send_list, send_smem, row_list, row_smem, flag_all,
     local_sem, meta_send, meta_recv, flag_send, flag_recv,
-    main_send, main_recv, side_send, side_recv, lent_sem, pack_send, pack_recv, extra_send, extra_recv,
+    main_send, main_recv, side_send, side_recv, lent_sem, pack_send, pack_recv, extra_send, extra_recv, out_sem,
 ):
     row_count, col_count, layer_count, group_count, per_row, padded = sizes
     n, width, tile, _ = tiles_ref.shape
@@ -775,7 +775,7 @@
         lent[m] = own_piece(send_smem[0, m])
         return carry
 
-    lax.fori_loop(0, per_lent, lent_pack, 0, unroll=4)
+    lax.fori_loop(0, per_lent, lent_pack, 0, unroll=8)
     lent_copy = remote(lent, borrowed, lent_sem.at[0], lent_sem.at[1], across)
     launch(lent_copy)
 
@@ -848,7 +848,7 @@
                 arrived[c, m] = plane_piece(at, m)
         return carry
 
-    lax.fori_loop(0, per_plane, plane_pack, 0, unroll=2)
+    lax.fori_loop(0, per_plane, plane_pack, 0, unroll=4)
 
     def pack_copy(offset, origin):
         return remote(
@@ -930,15 +930,20 @@
         extra[m, my_rows] = arrived[lax.div(code, per_plane), lax.rem(code, per_plane)]
         return carry
 
-    lax.fori_loop(0, pool, pool_pack, 0, unroll=4)
-
-    def extra_copy(way):
+    lax.fori_loop(0, pool, pool_pack, 0, unroll=8)
+
+    def extra_copy(way, half):
         device = (partner, facing, partner)[way]
-        piece = extra.at[:, pl.ds((facing_layer if way == 2 else l) * quarter, quarter)]
-        return remote(piece, piece, extra_send.at[way], extra_recv.at[way], device)
-
-    launch(extra_copy(0))
-    launch(extra_copy(1))
+        piece = extra.at[
+            pl.ds(half * (pool // 2), pool // 2),
+            pl.ds((facing_layer if way == 2 else l) * quarter, quarter),
+        ]
+        return remote(piece, piece, extra_send.at[way, half], extra_recv.at[way, half], device)
+
+    for half in range(2):
+        launch(extra_copy(1, half))
+    for half in range(2):
+        launch(extra_copy(0, half))
     for entry in line[:2]:
         take_wide(*entry)
     await_recv(line_copy(opposite, 2, 1))
@@ -969,31 +974,33 @@
         return carry
 
     lax.fori_loop(0, n, near_row, 0, unroll=2)
-    await_recv(extra_copy(1))
-    launch(extra_copy(2))
-    await_recv(extra_copy(0))
-    await_recv(extra_copy(2))
+    for half in range(2):
+        await_recv(extra_copy(1, half))
+        launch(extra_copy(2, half))
+    for half in range(2):
+        await_recv(extra_copy(0, half))
+        await_recv(extra_copy(2, half))
 
     def far_row(i, carry):
-        lefts, rights = [], []
+        values = [total[i, t * quarter:(t + 1) * quarter] for t in range(width)]
         for q in range(per_row):
             code = jnp.clip(row_smem[q, i], 0, pool * 256 - 1)
             goal = lax.rem(code, 16)
             at = jnp.minimum(lax.rem(lax.div(code, 16), 16), width - 1)
-            piece = left[i, at, my_rows]
-            lefts.append(jnp.concatenate(
-                [jnp.where(goal == t + 1, piece, jnp.zeros_like(piece)) for t in range(width)], axis=0
-            ))
-            rights.append(extra[lax.div(code, 256)])
-        value = total[i] + dot(
-            jnp.concatenate(lefts, axis=1), jnp.concatenate(rights, axis=0)
-        )
-        stage[i] = value.astype(stage.dtype).reshape(width, quarter, tile)
+            value = dot(left[i, at, my_rows], extra[lax.div(code, 256)])
+            values = [v + jnp.where(goal == t + 1, value, 0.0) for t, v in enumerate(values)]
+        for t in range(width):
+            stage[i, t] = values[t].astype(stage.dtype)
         return carry
 
-    lax.fori_loop(0, n, far_row, 0, unroll=8)
-    out_copy = pltpu.make_async_copy(stage, out_ref, local_sem.at[6])
-    out_copy.start()
+    out_copies = []
+    for chunk in range(n // 8):
+        lax.fori_loop(chunk * 8, chunk * 8 + 8, far_row, 0, unroll=8)
+        rows = pl.ds(chunk * 8, 8)
+        out_copies.append(pltpu.make_async_copy(
+            stage.at[rows], out_ref.at[rows], out_sem.at[chunk]
+        ))
+        out_copies[-1].start()
     for copy in flag_copies:
         copy.wait_recv()
     flag_ref[0, 0] = jnp.max(flag_all[...])
@@ -1006,7 +1013,8 @@
             @pl.when(condition)
             def _():
                 copy.wait_send()
-    out_copy.wait()
+    for copy in out_copies:
+        copy.wait()
 
 
 def on_device_sparse(density_tiles, tile_columns):
@@ -1069,8 +1077,9 @@
             pltpu.SemaphoreType.DMA((2,)),
             pltpu.SemaphoreType.DMA((col_count,)),
             pltpu.SemaphoreType.DMA((col_count,)),
-            pltpu.SemaphoreType.DMA((3,)),
-            pltpu.SemaphoreType.DMA((3,)),
+            pltpu.SemaphoreType.DMA((3, 2)),
+            pltpu.SemaphoreType.DMA((3, 2)),
+            pltpu.SemaphoreType.DMA((n // 8,)),
         ],
         compiler_params=pltpu.CompilerParams(
             collective_id=2, has_side_effects=True, vmem_limit_bytes=60 * 1024 * 1024

time: 60.1 us -> 59 us (0.982)
  Pallas kernels: 57.7 us -> 56.6 us
    pallas_call x1, Pallas kernels: 57.7 us -> 56.6 us  [on_device_sparse(): pl.pallas_call(functools.partial(sparse_kernel, sizes), out_shape=(jax.Sh...]
where the time goes in v3:
time: 59 us; the launch traced here: 58.4 us
  Pallas kernels  56.6 us (96%)
  local copies, waits for them, and re-layouts  1.15 us (2%)
  between operations  0.63 us (1%)
    pallas_call x1, Pallas kernels, on_device_sparse(): pl.pallas_call(functools.partial(sparse_kernel, sizes), out_shape=(jax.Sh...  56.6 us

profile of v3, /device:TPU:1, one launch (start us, length us, event | category | flops | bytes accessed | tf_op | source)
XLA Modules:
  0.0 58.4 jit_solution(6489222876151473509)
XLA Ops:
  0.0 0.0 copy-start
  0.0 56.6 %shard_map.30 = (bf16[24,8,32,128]{3,2,1,0:T(8,128)(2,1)S(1)}, s32[1,1]{1,0:T(1,128)}) custom-call(bf16[24,8,128,128]{3,2,1,0:T(8,128)(2,1)} %bitcast.7, s32[8,24]{1,0:T(8,128)} %bitcast.9), custom_call_target="tpu_custom_call" | custom-call | tf_op jit(solution)/shard_map/pallas_call | solution.py:1034
  57.2 0.0 copy-done
  57.3 1.1 %copy.11 = bf16[24,4,2,32,128]{4,3,2,1,0:T(8,128)(2,1)} copy(bf16[24,4,2,32,128]{4,3,2,1,0:T(8,128)(2,1)S(1)} %get-tuple-element.21) | data formatting | bytes 3145728
  (1 shorter events, 0.0 us)
Async XLA Ops:
  0.0 57.2 %copy-start = (s32[24,4,2]{0,2,1:T(2,128)S(1)}, s32[24,4,2]{0,2,1:T(2,128)}, u32[]{:S(2)}) copy-start(s32[24,4,2]{0,2,1:T(2,128)} %param.5) | copy-start | bytes 2308

commit v4 on v3

--- a/solution.py
+++ b/solution.py
@@ -802,7 +802,6 @@
 
     for entry in line[2:4]:
         take_line(*entry)
-    launch(line_copy(me, 2, 1))
 
     def plane_step(at, wanted):
         cell = r * col_count + at
@@ -865,6 +864,7 @@
 
     for entry in line[4:]:
         take_line(*entry)
+    launch(line_copy(me, 2, 1))
     for entry in beyond[:2]:
         take_beyond(*entry)
 

time: 59 us -> 59 us (level)
  no operation moved by 1% of the time
where the time goes in v4:
time: 59 us; the launch traced here: 58.4 us
  Pallas kernels  56.6 us (96%)
  local copies, waits for them, and re-layouts  1.15 us (2%)
  between operations  0.63 us (1%)
    pallas_call x1, Pallas kernels, on_device_sparse(): pl.pallas_call(functools.partial(sparse_kernel, sizes), out_shape=(jax.Sh...  56.6 us

profile of v4, /device:TPU:1, one launch (start us, length us, event | category | flops | bytes accessed | tf_op | source)
XLA Modules:
  0.0 58.4 jit_solution(17386927129863838195)
XLA Ops:
  0.0 0.0 copy-start
  0.0 56.6 %shard_map.30 = (bf16[24,8,32,128]{3,2,1,0:T(8,128)(2,1)S(1)}, s32[1,1]{1,0:T(1,128)}) custom-call(bf16[24,8,128,128]{3,2,1,0:T(8,128)(2,1)} %bitcast.7, s32[8,24]{1,0:T(8,128)} %bitcast.9), custom_call_target="tpu_custom_call" | custom-call | tf_op jit(solution)/shard_map/pallas_call | solution.py:1034
  57.2 0.0 copy-done
  57.3 1.1 %copy.11 = bf16[24,4,2,32,128]{4,3,2,1,0:T(8,128)(2,1)} copy(bf16[24,4,2,32,128]{4,3,2,1,0:T(8,128)(2,1)S(1)} %get-tuple-element.21) | data formatting | bytes 3145728
  (1 shorter events, 0.0 us)
Async XLA Ops:
  0.0 57.2 %copy-start = (s32[24,4,2]{0,2,1:T(2,128)S(1)}, s32[24,4,2]{0,2,1:T(2,128)}, u32[]{:S(2)}) copy-start(s32[24,4,2]{0,2,1:T(2,128)} %param.5) | copy-start | bytes 2308
